TPU v7x, 32 devices: a whole 2x2x4 slice. The times are simulated.
32 devices in a mesh: dp: 8 (over z, x), mp: 4 (over y, core).
Axes of the slice: x: 2, y: 2, z: 4, core: 2. Of those that a mesh axis runs over, the one named last changes fastest.
Arguments:
- activations: bfloat16 [1024, 1024], P('dp'), may hold values from -6 to 6
- cotangents: bfloat16 [1024, 4096], P('dp', 'mp'), may hold values from -1200 to 1200
- owners: int32 [4], replicated, may hold values from 0 to 7, as said below
Outputs:
- update: bfloat16 [1024, 4096], P('dp', 'mp')
- roots: float32 [4096, 2048], P('dp', 'mp')
- graft: float32 [], replicated
Inputs may be any that keep to these rules, and one draw needn't show every extreme that they name: The left root of block b is computed at dp index owners[b] and its right root at owners[b] with its lowest bit flipped; every dp index computes exactly one root.
All inputs are finite; a program needn't handle non-finite values.
Results may differ from a plain program's by a relative error of at most 0.00045.
Values may be sent and summed in bfloat16 or wider, within the bound.
No kernel may reach another device: no remote copies, remote signals or barrier semaphores. Data moves between devices by JAX's collectives and lax.ppermute only.
A program may use at most 64 MiB of HBM per device.

v0:
```python
import math
import jax
import jax.numpy as jnp
from jax import lax
from jax.sharding import PartitionSpec as P

B = 512
CB = 2
ITERS = 3


def partner_2(value, axis, bit):
    return lax.ppermute(value, axis, [(i, i ^ 1 << bit) for i in range(lax.axis_size(axis))])


def product(left, right):
    return jnp.dot(left, right, precision=lax.Precision.HIGHEST, preferred_element_type=jnp.float32)


def statistic_of(operand):
    gram = product(operand, operand.T)
    ridge = 0.1 * (jnp.sum(operand * operand) / operand.shape[0] + 1.0)
    return gram + ridge * jnp.eye(operand.shape[0], dtype=jnp.float32)


def inverse_root(statistic):
    eye_matrix = jnp.eye(statistic.shape[0], dtype=jnp.float32)
    magnitude = jnp.sqrt(jnp.sum(statistic * statistic))
    current = statistic / magnitude
    result = eye_matrix
    for step in range(ITERS):
        factor = (5.0 * eye_matrix - current) * 0.25
        if step == 0:
            result = factor * magnitude ** (-0.25)
        else:
            result = product(result, factor)
        if step + 1 < ITERS:
            square = product(factor, factor)
            current = product(product(square, square), current)
    return result


def half_squares(matrix, upper_half):
    row_ids = jnp.arange(matrix.shape[0], dtype=jnp.int32)
    in_half = (row_ids < matrix.shape[0] // 2) == upper_half
    return jnp.sum(jnp.where(in_half[:, None], matrix * matrix, 0.0), axis=0)


def on_device(activations, cotangents, owners):
    my_index = lax.axis_index("dp")
    dp_count = lax.axis_size("dp")
    local_tokens = activations.shape[0]
    row_blocks = activations.shape[1] // B
    block_count = owners.shape[0]
    dest_index = jnp.arange(dp_count, dtype=jnp.int32)
    partner = owners + 1 - 2 * (owners % 2)
    left_match = owners[None, :] == dest_index[:, None]
    right_match = partner[None, :] == dest_index[:, None]
    block_ids = jnp.arange(block_count, dtype=jnp.int32)
    owned = jnp.sum(jnp.where(left_match | right_match, block_ids[None, :], 0), axis=1)
    left_dest = jnp.any(left_match, axis=1)
    row_dest = owned // CB
    col_dest = owned % CB
    my_block = owned[my_index]
    my_left = left_dest[my_index]
    token_rows = jnp.take(activations.reshape(local_tokens, row_blocks, B), row_dest, axis=1)
    cotangent_rows = jnp.take(cotangents.reshape(local_tokens, CB, B), col_dest, axis=1)
    mixed = jnp.where(left_dest[None, :, None], token_rows, cotangent_rows)
    received = lax.all_to_all(mixed, "dp", split_axis=1, concat_axis=0, tiled=True)[:, 0, :]
    partner_part = partner_2(received, "dp", 0)
    inputs_block = jnp.where(my_left, received, partner_part)
    outputs_block = jnp.where(my_left, partner_part, received)
    all_tokens = inputs_block.shape[0]
    gradient = lax.dot_general(
        inputs_block, outputs_block, (((0,), (0,)), ((), ())), preferred_element_type=jnp.float32
    ) / math.sqrt(all_tokens)
    grad_share = half_squares(gradient, my_left)
    grad_total = jnp.sum(lax.psum(grad_share, ("dp", "mp")))
    oriented = jnp.where(my_left, gradient, gradient.T)
    root = inverse_root(statistic_of(oriented))
    other_root = partner_2(root, "dp", 0)
    left_root = jnp.where(my_left, root, other_root)
    right_root = jnp.where(my_left, other_root, root)
    preconditioned = product(left_root, product(gradient, right_root))
    precond_share = half_squares(preconditioned, my_left)
    precond_total = jnp.sum(lax.psum(precond_share, ("dp", "mp")))
    graft = jnp.sqrt(grad_total / jnp.maximum(precond_total, 1.0))
    scaled = jnp.where(my_left, graft * preconditioned, 0.0).astype(jnp.bfloat16)
    dest_rows = activations.shape[1] // dp_count
    pieces = scaled.reshape(B // dest_rows, dest_rows, B)
    outgoing = jnp.zeros((dp_count, dest_rows, B), jnp.bfloat16)
    first_dest = my_block // CB * (B // dest_rows)
    outgoing = lax.dynamic_update_slice(outgoing, pieces, (first_dest, jnp.int32(0), jnp.int32(0)))
    incoming = lax.all_to_all(outgoing, "dp", split_axis=0, concat_axis=0, tiled=True)
    selector = (
        (col_dest[:, None] == jnp.arange(CB, dtype=jnp.int32)[None, :]) & left_dest[:, None]
    ).astype(jnp.bfloat16)
    update = jnp.einsum("srb,sc->rcb", incoming, selector, preferred_element_type=jnp.float32)
    update = update.reshape(dest_rows, CB * B).astype(jnp.bfloat16)
    return (update, root, graft)


def solution(mesh):
    return jax.shard_map(
        on_device,
        mesh=mesh,
        in_specs=(P("dp", None), P("dp", "mp"), P()),
        out_specs=(P("dp", "mp"), P("dp", "mp"), P()),
        check_vma=False,
    )
```

profile of v0, /device:TPU:0, one launch (start us, length us, event | category | flops | bytes accessed | tf_op | source)
XLA Modules:
  0.0 190.2 jit_solution(12887503934430091397)
XLA Ops:
  0.6 0.7 fusion.38
  1.6 1.1 copy.24
  2.9 0.8 copy-done.3
  4.0 0.6 gather_fusion.1
  4.6 0.6 gather_fusion
  5.5 32.8 %all_to_all.20 = bf16[128,8,512]{2,0,1:T(8,128)(2,1)S(1)} all-to-all(bf16[128,8,512]{2,0,1:T(8,128)(2,1)S(1)} %bitcast_select_fusion.1), channel_id=1, replica_groups=mesh['dp'=8,'mp'=4] {'dp'}, dimensions={1} | all-to-all | bytes 2097152 | tf_op jit(solution)/shard_map/all_to_all | solution.py:69
  38.3 1.4 collective-permute-start
  39.8 0.6 dynamic_slice.6
  40.3 0.7 fusion.31
  41.0 21.1 %collective-permute-done = bf16[1024,512]{1,0:T(8,128)(2,1)S(1)} collective-permute-done((bf16[1024,512]{1,0:T(8,128)(2,1)S(1)}, bf16[1024,512]{1,0:T(8,128)(2,1)S(1)}, u32[]{:S(2)}, u32[]{:S(2)}) %collective-permute-start) | collective-permute-done | bytes 1048608 | tf_op jit(solution)/shard_map/ppermute | solution.py:13
  62.1 1.4 convolution_multiply_fusion
  63.8 1.6 select_reduce_fusion.1
  66.0 3.3 %multiply_reduce_fusion = (f32[]{:T(128)}, f32[512,512]{1,0:T(8,128)S(1)}) fusion(f32[]{:T(128)S(6)} %mul_shard_map.3, f32[512,512]{1,0:T(8,128)S(1)} %convolution_multiply_fusion, f32[512,512]{0,1:T(8,128)S(1)} %copy.26, pred[]{:T(512)} %bitcast.1), kind=kOutput, calls=%fused_computation.23 | convolution fusion | flops 1612185600 | bytes 3145737 | tf_op jit(solution)/shard_map/dot_general | solution.py:17
  70.0 2.0 %fusion.7 = f32[512,512]{1,0:T(8,128)S(1)} fusion(f32[512,512]{1,0:T(8,128)S(1)} %get-tuple-element.15, f32[]{:T(128)S(6)} %sqrt.6), kind=kOutput, calls=%fused_computation.19 | convolution fusion | flops 1611923456 | bytes 2097156 | tf_op jit(solution)/shard_map/dot_general | solution.py:17
  72.0 1.8 fusion.51
  73.8 1.9 fusion.50
  75.7 1.9 %fusion.14 = f32[512,512]{1,0:T(8,128)S(1)} fusion(f32[512,512]{1,0:T(8,128)S(1)} %fusion.50), kind=kOutput, calls=%fused_computation.30 | convolution fusion | flops 1611661312 | bytes 2097152 | tf_op jit(solution)/shard_map/dot_general | solution.py:17
  77.6 1.8 fusion.52
  79.5 2.0 %fusion = f32[512,512]{1,0:T(8,128)S(1)} fusion(f32[512,512]{1,0:T(8,128)S(1)} %fusion.52, f32[512,512]{1,0:T(8,128)S(1)} %fusion.50), kind=kOutput, calls=%fused_computation.7 | convolution fusion | flops 1611661312 | bytes 3145728 | tf_op jit(solution)/shard_map/dot_general | solution.py:17
  81.6 3.5 %fusion.9 = f32[512,512]{1,0:T(8,128)S(1)} fusion(f32[512,512]{1,0:T(8,128)} %copy-done.1, f32[]{:T(128)S(6)} %mul.63, f32[512,512]{1,0:T(8,128)} %copy-done.2, f32[]{:T(128)S(6)} %sqrt.6), kind=kOutput, calls=%fused_computation.21 | convolution fusion | flops 1612972032 | bytes 3145736 | tf_op jit(solution)/shard_map/dot_general | solution.py:17
  85.2 1.8 fusion.53
  87.0 1.6 collective-permute-start.1
  91.8 18.1 %collective-permute-done.1 = f32[512,512]{1,0:T(8,128)S(1)} collective-permute-done((f32[512,512]{1,0:T(8,128)S(1)}, f32[512,512]{1,0:T(8,128)S(1)}, u32[]{:S(2)}, u32[]{:S(2)}) %collective-permute-start.1) | collective-permute-done | bytes 1048608 | tf_op jit(solution)/shard_map/ppermute | solution.py:13
  110.0 2.5 %fusion.3 = f32[512,512]{1,0:T(8,128)S(1)} fusion(f32[512,512]{1,0:T(8,128)S(1)} %convolution_multiply_fusion, f32[512,512]{1,0:T(8,128)S(1)} %collective-permute-done.1, f32[512,512]{1,0:T(8,128)S(1)} %fusion.53, pred[]{:T(512)} %bitcast.1), kind=kOutput, calls=%fused_computation.15 | convolution fusion | flops 1610874880 | bytes 4194305 | tf_op jit(solution)/shard_map/dot_general | solution.py:17
  112.5 2.5 %select_reduce_fusion = (f32[512]{0:T(512)S(1)}, f32[512,512]{1,0:T(8,128)S(1)}) fusion(pred[512]{0:T(512)(128)(4,1)S(1)} %fusion.31, f32[512,512]{1,0:T(8,128)S(1)} %fusion.3, f32[512,512]{1,0:T(8,128)S(1)} %fusion.53, f32[512,512]{1,0:T(8,128)S(1)} %collective-permute-done.1, pred[]{:T(512)} %bitcast.1), kind=kOutput, calls=%fused_computation.14 | convolution fusion | flops 1611660800 | bytes 4196865 | tf_op jit(solution)/shard_map/dot_general | solution.py:17
  115.0 39.3 %all-reduce = (f32[512]{0:T(512)S(1)}, f32[512]{0:T(512)S(1)}) all-reduce(f32[512]{0:T(512)S(1)} %get-tuple-element.4, f32[512]{0:T(512)S(1)} %get-tuple-element.16), channel_id=1, replica_groups=mesh['dp'=8,'mp'=4] {'dp','mp'}, use_global_device_ids=true, to_apply=%region_3.5 | all-reduce | flops 1024 | bytes 8192 | tf_op jit(solution)/shard_map/psum | solution.py:78
  154.4 0.6 reduce_sum.69
  155.6 0.6 reduce_sum.65
  156.9 0.8 select_convert_fusion
  157.8 29.7 %all_to_all.21 = bf16[8,128,512]{2,1,0:T(8,128)(2,1)S(1)} all-to-all(bf16[8,128,512]{2,1,0:T(8,128)(2,1)S(1)} %constant_dynamic-update-slice_fusion), channel_id=1, replica_groups=mesh['dp'=8,'mp'=4] {'dp'}, dimensions={0} | all-to-all | bytes 2097152 | tf_op jit(solution)/shard_map/all_to_all | solution.py:94
  187.6 0.7 convolution_convert_fusion
  188.3 0.7 copy.28
  (23 shorter events, 2.0 us)
Async XLA Ops:
  0.6 0.7 copy-start.4
  2.7 1.0 copy-start.3
  38.3 23.7 %collective-permute-start = (bf16[1024,512]{1,0:T(8,128)(2,1)S(1)}, bf16[1024,512]{1,0:T(8,128)(2,1)S(1)}, u32[]{:S(2)}, u32[]{:S(2)}) collective-permute-start(bf16[1024,512]{1,0:T(8,128)(2,1)S(1)} %bitcast.39), channel_id=1, source_target_pairs={{0,4},{4,0},{8,12},{12,8},{16,20},{20,16},{24,28},{28,24},{1,5},{5... | collective-permute-start | bytes 3145736 | tf_op jit(solution)/shard_map/ppermute | solution.py:13
  69.3 4.5 %copy-start.2 = (f32[512,512]{1,0:T(8,128)}, f32[512,512]{1,0:T(8,128)S(1)}, u32[]{:S(2)}) copy-start(f32[512,512]{1,0:T(8,128)S(1)} %get-tuple-element.15) | copy-start | bytes 3145732
  75.7 3.8 %copy-start.1 = (f32[512,512]{1,0:T(8,128)}, f32[512,512]{1,0:T(8,128)S(1)}, u32[]{:S(2)}) copy-start(f32[512,512]{1,0:T(8,128)S(1)} %fusion.50) | copy-start | bytes 3145732
  87.0 25.5 %copy-start = (f32[512,512]{1,0:T(8,128)}, f32[512,512]{1,0:T(8,128)S(1)}, u32[]{:S(2)}) copy-start(f32[512,512]{1,0:T(8,128)S(1)} %fusion.53) | copy-start | bytes 3145732
  87.0 22.9 %collective-permute-start.1 = (f32[512,512]{1,0:T(8,128)S(1)}, f32[512,512]{1,0:T(8,128)S(1)}, u32[]{:S(2)}, u32[]{:S(2)}) collective-permute-start(f32[512,512]{1,0:T(8,128)S(1)} %fusion.53), channel_id=1, source_target_pairs={{0,4},{4,0},{8,12},{12,8},{16,20},{20,16},{24,28},{28,24},{1,5},{5... | collective-permute-start | bytes 3145736 | tf_op jit(solution)/shard_map/ppermute | solution.py:13
where the time goes:
time: 191 us; the launch traced here: 190 us
  blocking collectives  102 us (53%)
  waiting for transfers between devices  39.2 us (21%)
  matrix products  27.3 us (14%)
  between operations  7.38 us (4%)
  local copies, waits for them, and re-layouts  5.98 us (3%)
  other arithmetic  5.36 us (3%)
  starting transfers between devices  3.01 us (2%)
    psum x1, blocking collectives, on_device(): grad_total = jnp.sum(lax.psum(grad_share, ('dp', 'mp')))  39.3 us
    ppermute x2, waiting for transfers between devices, partner_2(): lax.ppermute(value, axis, [(i, i ^ 1 << bit) for i in range(lax.axis_size...  39.2 us
    all_to_all x1, blocking collectives, on_device(): lax.all_to_all(mixed, 'dp', split_axis=1, concat_axis=0, tiled=True)  32.8 us
    all_to_all x1, blocking collectives, on_device(): lax.all_to_all(outgoing, 'dp', split_axis=0, concat_axis=0, tiled=True)  29.7 us
    dot_general x11, matrix products, product(): jnp.dot(left, right, precision=lax.Precision.HIGHEST, preferred_element_t...  25.2 us
  transfers between devices with their start and end apart: 2, of which 2 were waited for; matrix products, arithmetic and copies ran while one was open for 1% of the time, Pallas kernels for 0%

commit v1 on v0

--- a/solution.py
+++ b/solution.py
@@ -75,7 +75,7 @@
         inputs_block, outputs_block, (((0,), (0,)), ((), ())), preferred_element_type=jnp.float32
     ) / math.sqrt(all_tokens)
     grad_share = half_squares(gradient, my_left)
-    grad_total = jnp.sum(lax.psum(grad_share, ("dp", "mp")))
+    grad_total = jnp.sum(lax.psum(lax.psum(grad_share, "mp"), "dp"))
     oriented = jnp.where(my_left, gradient, gradient.T)
     root = inverse_root(statistic_of(oriented))
     other_root = partner_2(root, "dp", 0)

time: 191 us -> 203 us (1.063)
  blocking collectives: 102 us -> 132 us
  waiting for transfers between devices: 39.2 us -> 21.1 us
    psum x1 -> x3, blocking collectives: 39.3 us -> 68.8 us  [the longest x1 36.9 us: on_device(): precond_total = jnp.sum(lax.psum(precond_share, ('dp', 'mp')))]
    ppermute x2, waiting for transfers between devices: 39.2 us -> 21.1 us  [partner_2(): lax.ppermute(value, axis, [(i, i ^ 1 << bit) for i in range(lax.axis_size...]
  transfers between devices with their start and end apart: 2 -> 2, of which waited for: 2 -> 1; matrix products, arithmetic and copies ran while one was open for 1% -> 1% of each run, Pallas kernels for 0% -> 0%
where the time goes in v1:
time: 203 us
  blocking collectives  132 us (65%)
  matrix products  27.3 us (13%)
  waiting for transfers between devices  21.1 us (10%)
  between operations  7.42 us (4%)
  local copies, waits for them, and re-layouts  5.98 us (3%)
  other arithmetic  5.45 us (3%)
  starting transfers between devices  3.01 us (1%)
    psum x1, blocking collectives, on_device(): precond_total = jnp.sum(lax.psum(precond_share, ('dp', 'mp')))  36.9 us
    all_to_all x1, blocking collectives, on_device(): lax.all_to_all(mixed, 'dp', split_axis=1, concat_axis=0, tiled=True)  32.8 us
    psum x2, blocking collectives, on_device(): grad_total = jnp.sum(lax.psum(lax.psum(grad_share, 'mp'), 'dp'))  31.9 us
    all_to_all x1, blocking collectives, on_device(): lax.all_to_all(outgoing, 'dp', split_axis=0, concat_axis=0, tiled=True)  30.8 us
    dot_general x11, matrix products, product(): jnp.dot(left, right, precision=lax.Precision.HIGHEST, preferred_element_t...  25.2 us
    ppermute x2, waiting for transfers between devices, partner_2(): lax.ppermute(value, axis, [(i, i ^ 1 << bit) for i in range(lax.axis_size...  21.1 us
  transfers between devices with their start and end apart: 2, of which 1 were waited for; matrix products, arithmetic and copies ran while one was open for 1% of the time, Pallas kernels for 0%

profile of v1, /device:TPU:0, one launch (start us, length us, event | category | flops | bytes accessed | tf_op | source)
XLA Modules:
  0.0 202.7 jit_solution(10443683498046460602)
XLA Ops:
  0.6 0.7 fusion.38
  1.6 1.1 copy.24
  2.9 0.8 copy-done.3
  4.0 0.6 gather_fusion.1
  4.6 0.6 gather_fusion
  5.5 32.8 %all_to_all.20 = bf16[128,8,512]{2,0,1:T(8,128)(2,1)S(1)} all-to-all(bf16[128,8,512]{2,0,1:T(8,128)(2,1)S(1)} %bitcast_select_fusion.1), channel_id=1, replica_groups=mesh['dp'=8,'mp'=4] {'dp'}, dimensions={1} | all-to-all | bytes 2097152 | tf_op jit(solution)/shard_map/all_to_all | solution.py:69
  38.3 1.4 collective-permute-start
  40.3 0.7 fusion.31
  41.0 21.1 %collective-permute-done = bf16[1024,512]{1,0:T(8,128)(2,1)S(1)} collective-permute-done((bf16[1024,512]{1,0:T(8,128)(2,1)S(1)}, bf16[1024,512]{1,0:T(8,128)(2,1)S(1)}, u32[]{:S(2)}, u32[]{:S(2)}) %collective-permute-start) | collective-permute-done | bytes 1048608 | tf_op jit(solution)/shard_map/ppermute | solution.py:13
  62.1 1.4 convolution_multiply_fusion
  63.8 1.6 select_reduce_fusion.1
  66.0 3.3 %multiply_reduce_fusion = (f32[]{:T(128)}, f32[512,512]{1,0:T(8,128)S(1)}) fusion(f32[]{:T(128)S(6)} %mul_shard_map.3, f32[512,512]{1,0:T(8,128)S(1)} %convolution_multiply_fusion, f32[512,512]{0,1:T(8,128)S(1)} %copy.26, pred[]{:T(512)} %bitcast.1), kind=kOutput, calls=%fused_computation.23 | convolution fusion | flops 1612185600 | bytes 3145737 | tf_op jit(solution)/shard_map/dot_general | solution.py:17
  70.0 2.0 fusion.7
  72.0 1.8 fusion.51
  73.8 1.9 fusion.50
  75.7 1.9 fusion.14
  77.6 1.8 fusion.52
  79.5 2.0 %fusion = f32[512,512]{1,0:T(8,128)S(1)} fusion(f32[512,512]{1,0:T(8,128)S(1)} %fusion.52, f32[512,512]{1,0:T(8,128)S(1)} %fusion.50), kind=kOutput, calls=%fused_computation.7 | convolution fusion | flops 1611661312 | bytes 3145728 | tf_op jit(solution)/shard_map/dot_general | solution.py:17
  81.6 3.5 %fusion.9 = f32[512,512]{1,0:T(8,128)S(1)} fusion(f32[512,512]{1,0:T(8,128)} %copy-done.1, f32[]{:T(128)S(6)} %mul.63, f32[512,512]{1,0:T(8,128)} %copy-done.2, f32[]{:T(128)S(6)} %sqrt.6), kind=kOutput, calls=%fused_computation.21 | convolution fusion | flops 1612972032 | bytes 3145736 | tf_op jit(solution)/shard_map/dot_general | solution.py:17
  85.2 1.8 fusion.53
  87.0 1.6 collective-permute-start.1
  91.8 6.0 %psum.21 = f32[512]{0:T(512)S(1)} all-reduce(f32[512]{0:T(512)S(1)} %get-tuple-element.4), channel_id=1, replica_groups=mesh['dp'=8,'mp'=4] {'mp'}, use_global_device_ids=true, to_apply=%region_3.5 | all-reduce | flops 512 | bytes 4096 | tf_op jit(solution)/shard_map/psum | solution.py:78
  97.8 25.9 %psum.22 = f32[512]{0:T(512)S(1)} all-reduce(f32[512]{0:T(512)S(1)} %psum.21), channel_id=1, replica_groups=mesh['dp'=8,'mp'=4] {'dp'}, use_global_device_ids=true, to_apply=%region_4.6 | all-reduce | flops 512 | bytes 4096 | tf_op jit(solution)/shard_map/psum | solution.py:78
  123.7 0.6 reduce_sum.65
  124.3 2.5 %fusion.3 = f32[512,512]{1,0:T(8,128)S(1)} fusion(f32[512,512]{1,0:T(8,128)S(1)} %convolution_multiply_fusion, f32[512,512]{1,0:T(8,128)S(1)} %collective-permute-done.1, f32[512,512]{1,0:T(8,128)S(1)} %fusion.53, pred[]{:T(512)} %bitcast.1), kind=kOutput, calls=%fused_computation.15 | convolution fusion | flops 1610874880 | bytes 4194305 | tf_op jit(solution)/shard_map/dot_general | solution.py:17
  126.9 2.5 %select_reduce_fusion = (f32[512]{0:T(512)S(1)}, f32[512,512]{1,0:T(8,128)S(1)}) fusion(pred[512]{0:T(512)(128)(4,1)S(1)} %fusion.31, f32[512,512]{1,0:T(8,128)S(1)} %fusion.3, f32[512,512]{1,0:T(8,128)S(1)} %fusion.53, f32[512,512]{1,0:T(8,128)S(1)} %collective-permute-done.1, pred[]{:T(512)} %bitcast.1), kind=kOutput, calls=%fused_computation.14 | convolution fusion | flops 1611660800 | bytes 4196865 | tf_op jit(solution)/shard_map/dot_general | solution.py:17
  129.4 36.9 %psum.23 = f32[512]{0:T(512)S(1)} all-reduce(f32[512]{0:T(512)S(1)} %get-tuple-element.14), channel_id=1, replica_groups=mesh['dp'=8,'mp'=4] {'dp','mp'}, use_global_device_ids=true, to_apply=%region_9.11 | all-reduce | flops 512 | bytes 4096 | tf_op jit(solution)/shard_map/psum | solution.py:86
  166.3 0.7 reduce_sum.69
  168.3 0.8 select_convert_fusion
  169.3 30.8 %all_to_all.21 = bf16[8,128,512]{2,1,0:T(8,128)(2,1)S(1)} all-to-all(bf16[8,128,512]{2,1,0:T(8,128)(2,1)S(1)} %constant_dynamic-update-slice_fusion), channel_id=1, replica_groups=mesh['dp'=8,'mp'=4] {'dp'}, dimensions={0} | all-to-all | bytes 2097152 | tf_op jit(solution)/shard_map/all_to_all | solution.py:94
  200.0 0.7 convolution_convert_fusion
  200.8 0.7 copy.28
  (25 shorter events, 2.6 us)
Async XLA Ops:
  0.6 0.7 copy-start.4
  2.7 1.0 copy-start.3
  38.3 23.7 %collective-permute-start = (bf16[1024,512]{1,0:T(8,128)(2,1)S(1)}, bf16[1024,512]{1,0:T(8,128)(2,1)S(1)}, u32[]{:S(2)}, u32[]{:S(2)}) collective-permute-start(bf16[1024,512]{1,0:T(8,128)(2,1)S(1)} %bitcast.39), channel_id=1, source_target_pairs={{0,4},{4,0},{8,12},{12,8},{16,20},{20,16},{24,28},{28,24},{1,5},{5... | collective-permute-start | bytes 3145736 | tf_op jit(solution)/shard_map/ppermute | solution.py:13
  69.3 4.5 %copy-start.2 = (f32[512,512]{1,0:T(8,128)}, f32[512,512]{1,0:T(8,128)S(1)}, u32[]{:S(2)}) copy-start(f32[512,512]{1,0:T(8,128)S(1)} %get-tuple-element.13) | copy-start | bytes 3145732
  75.7 3.8 %copy-start.1 = (f32[512,512]{1,0:T(8,128)}, f32[512,512]{1,0:T(8,128)S(1)}, u32[]{:S(2)}) copy-start(f32[512,512]{1,0:T(8,128)S(1)} %fusion.50) | copy-start | bytes 3145732
  87.0 39.8 %copy-start = (f32[512,512]{1,0:T(8,128)}, f32[512,512]{1,0:T(8,128)S(1)}, u32[]{:S(2)}) copy-start(f32[512,512]{1,0:T(8,128)S(1)} %fusion.53) | copy-start | bytes 3145732
  87.0 37.3 %collective-permute-start.1 = (f32[512,512]{1,0:T(8,128)S(1)}, f32[512,512]{1,0:T(8,128)S(1)}, u32[]{:S(2)}, u32[]{:S(2)}) collective-permute-start(f32[512,512]{1,0:T(8,128)S(1)} %fusion.53), channel_id=1, source_target_pairs={{0,4},{4,0},{8,12},{12,8},{16,20},{20,16},{24,28},{28,24},{1,5},{5... | collective-permute-start | bytes 3145736 | tf_op jit(solution)/shard_map/ppermute | solution.py:13
